TPU v7x, 32 devices: a whole 2x2x4 slice. The times are simulated.
32 devices in a mesh: grp: 2 (over y), seq: 4 (over z), head: 2 (over x), rep: 2 (over core).
Axes of the slice: x: 2, y: 2, z: 4, core: 2. Of those that a mesh axis runs over, the one named last changes fastest.
Arguments:
- x_proj: bfloat16 [4, 4, 4, 32, 8192], P(('grp', 'rep'), None, 'seq', None, 'head'), parts along dimension 0, may hold values from -6 to 6
- gate_proj: bfloat16 [4, 4, 4, 32, 8192], P(('grp', 'rep'), None, 'seq', None, 'head'), parts along dimension 0, may hold values from -6 to 6
- bc_proj: bfloat16 [4, 4, 4, 32, 256], P(('grp', 'rep'), None, 'seq'), parts along dimension 0, may hold values from -6 to 6
- dt_proj: bfloat16 [4, 4, 4, 32, 128], P(('grp', 'rep'), None, 'seq', None, 'head'), parts along dimension 0, may hold values from -5.5 to 7.5
- a_rate: float32 [128], P('head'), may hold values from 0.0001953125 to 0.05
- dt_bias: float32 [128], P('head'), may hold values from -1 to 1
- d_skip: float32 [128], P('head'), may hold values from 0.5 to 1.5
- conv_x_weight: float32 [4, 8192], P(None, 'head'), may hold values from -3 to 3
- conv_bc_weight: float32 [4, 256], replicated, may hold values from -3 to 3
- norm_gain: float32 [8192], P('head'), may hold values from 0.1 to 1.9
- out_weight: bfloat16 [8192, 2048], P(('seq', 'rep'), 'head'), may hold values from -0.0625 to 0.0625
- request_first_position: int32 [4], P(('grp', 'rep')), parts along dimension 0, may hold values from 0 to 255
- owner: int32 [4, 4], P(('grp', 'rep')), parts along dimension 0, may hold values from 0 to 3, each once within a row
Outputs:
- mixed: bfloat16 [4, 512, 2048], P(('grp', 'rep'), 'seq', 'head'), parts along dimension 0
- ssm_state: float32 [4, 4, 128, 2048], P(('grp', 'rep'), 'seq', 'head'), parts along dimension 0
- conv_x_state: bfloat16 [4, 4, 3, 2048], P(('grp', 'rep'), 'seq', None, 'head'), parts along dimension 0
- conv_bc_state: bfloat16 [4, 4, 3, 64], P(('grp', 'rep'), 'seq'), parts along dimension 0
There are 2 independent parts, one for each index of `grp`. A program takes and returns all parts, laid end to end along the dimension named above; an argument that names none is the same for every part. Nothing has to cross between parts.
Inputs may be any that keep to these rules, and one draw needn't show every extreme that they name: Each row of owner names every index of seq once.
All inputs are finite; a program needn't handle non-finite values.
Results may differ from a plain program's by a relative error of at most 0.007.
Values may be sent and summed in bfloat16 or wider, within the bound.
A program may use at most 128 MiB of HBM per device.

v0:
```python
import jax
import jax.numpy as jnp
from jax import lax
from jax.sharding import PartitionSpec as P

HEAD_DIM = 64
NSTATE = 128
KCONV = 4
SPAN = 128
INNER = 8192


highest = lax.Precision.HIGHEST
stability_constant = 1e-05


def passed_along(value, axis, by):
    devices = lax.axis_size(axis)
    pairs = [(i, i + by) for i in range(devices) if 0 <= i + by < devices]
    return lax.ppermute(value, axis, pairs)


def prefix(value, axis, combine, identity, reverse):
    devices, place = (lax.axis_size(axis), lax.axis_index(axis))
    everything = jax.tree.map(lambda part: lax.all_gather(part, axis), value)
    start = jax.tree.map(
        lambda part, zero: jnp.broadcast_to(jnp.asarray(zero, part.dtype), part.shape),
        value,
        identity,
    )

    def lap(k, before):
        at = devices - 1 - k if reverse else k
        reached = at > place if reverse else at < place
        new = combine(before, jax.tree.map(lambda part: part[at], everything))
        return jax.tree.map(lambda a, b: jnp.where(reached, a, b), new, before)

    return lax.fori_loop(0, devices, lap, start)


def broadcast(block, axis, source):
    block = jnp.where(lax.axis_index(axis) == source, block, jnp.zeros_like(block))
    return lax.psum(block, axis)


def span_terms(x_conv, b_rows, c_rows, step_size, log_decay):
    cum_decay = jnp.cumsum(log_decay, axis=1)
    scores = jnp.einsum("kqn,ktn->kqt", c_rows, b_rows, preferred_element_type=jnp.float32)
    cum_heads = jnp.swapaxes(cum_decay, 1, 2)
    step_heads = jnp.swapaxes(step_size, 1, 2)
    block_len = cum_decay.shape[1]
    causal = jnp.arange(block_len)[:, None] >= jnp.arange(block_len)[None, :]
    decay_gap = cum_heads[:, :, :, None] - cum_heads[:, :, None, :]
    seg_decay = jnp.exp(jnp.where(causal, decay_gap, -jnp.inf))
    weights = (scores[:, None] * seg_decay * step_heads[:, :, None, :]).astype(jnp.bfloat16)
    y_intra = jnp.einsum("khqt,kthp->kqhp", weights, x_conv, preferred_element_type=jnp.float32)
    remaining_length = jnp.exp(cum_decay[:, -1:, :] - cum_decay)
    scaled = ((remaining_length * step_size)[..., None] * x_conv.astype(jnp.float32)).astype(
        jnp.bfloat16
    )
    states = jnp.einsum("kthp,ktn->khpn", scaled, b_rows, preferred_element_type=jnp.float32)
    return (cum_decay, y_intra, states, jnp.exp(cum_decay[:, -1, :]))


def conv_silu(preceding_tokens, current, weight):
    extended = jnp.concatenate([preceding_tokens, current], axis=0)
    length = current.shape[0]
    accum = jnp.zeros(current.shape, jnp.float32)
    for offset in range(weight.shape[0]):
        accum = accum + weight[offset] * extended[offset : offset + length].astype(jnp.float32)
    return jax.nn.silu(accum)


def link(preceding_tokens, later):
    return (
        preceding_tokens[0] * later[0],
        later[0][:, None, None] * preceding_tokens[1] + later[1],
    )


def multiply(preceding_tokens, later):
    return preceding_tokens * later


def add_rows(source, piece):
    return jnp.dot(source, piece, preferred_element_type=jnp.float32)


def take_slab(values, slab_index, seq_count):
    grouped = values.reshape(values.shape[0], seq_count, -1)
    return lax.dynamic_index_in_dim(grouped, slab_index, axis=1, keepdims=False)


def local(
    x_proj,
    gate_proj,
    bc_proj,
    dt_proj,
    a_rate,
    dt_bias,
    d_skip,
    conv_x_weight,
    conv_bc_weight,
    norm_gain,
    out_weight,
    request_first_position,
    owner,
):
    x_all, z_all, bc_all, dt_all = (
        lax.all_to_all(x_proj, "seq", split_axis=1, concat_axis=2, tiled=True),
        lax.all_to_all(gate_proj, "seq", split_axis=1, concat_axis=2, tiled=True),
        lax.all_to_all(bc_proj, "seq", split_axis=1, concat_axis=2, tiled=True),
        lax.all_to_all(dt_proj, "seq", split_axis=1, concat_axis=2, tiled=True),
    )
    tokens_here = x_all.shape[2] * x_all.shape[3]
    x_local = x_all.reshape(tokens_here, x_all.shape[4])
    z_local = z_all.reshape(tokens_here, z_all.shape[4])
    bc_local = bc_all.reshape(tokens_here, bc_all.shape[4])
    dt_local = dt_all.reshape(tokens_here, dt_all.shape[4])
    heads = dt_local.shape[1]
    seq_index = lax.axis_index("seq")
    seq_count = lax.axis_size("seq")
    positions = seq_index * tokens_here + jnp.arange(tokens_here, dtype=jnp.int32)
    is_live = positions >= request_first_position[0]
    x_live = jnp.where(is_live[:, None], x_local, jnp.zeros_like(x_local))
    bc_live = jnp.where(is_live[:, None], bc_local, jnp.zeros_like(bc_local))
    rim_rows = KCONV - 1
    tail_x = x_live[tokens_here - rim_rows :]
    tail_bc = bc_live[tokens_here - rim_rows :]
    before_x, before_bc = passed_along((tail_x, tail_bc), "seq", 1)
    x_conv = conv_silu(before_x, x_live, conv_x_weight).astype(jnp.bfloat16)
    bc_conv = conv_silu(before_bc, bc_live, conv_bc_weight).astype(jnp.bfloat16)
    step_size = (
        jax.nn.softplus(dt_local.astype(jnp.float32) + dt_bias)
        * is_live.astype(jnp.float32)[:, None]
    )
    log_decay = -a_rate * step_size
    blocks = tokens_here // SPAN
    x_blocks = x_conv.reshape(blocks, SPAN, heads, HEAD_DIM)
    b_blocks = bc_conv[:, :NSTATE].reshape(blocks, SPAN, NSTATE)
    c_blocks = bc_conv[:, NSTATE:].reshape(blocks, SPAN, NSTATE)
    cum_decay, y_intra, states, decays = span_terms(
        x_blocks,
        b_blocks,
        c_blocks,
        step_size.reshape(blocks, SPAN, heads),
        log_decay.reshape(blocks, SPAN, heads),
    )

    def advance(carry, inputs):
        factor, contrib = inputs
        return (factor[:, None, None] * carry + contrib, carry)

    zero_state = jnp.zeros((heads, HEAD_DIM, NSTATE), jnp.float32)
    local_final, local_enter = lax.scan(advance, zero_state, (decays, states))
    dev_decay = jnp.prod(decays, axis=0)
    ones_heads = jnp.ones((heads,), jnp.float32)
    enter_decay, enter_state = prefix(
        (dev_decay, local_final), "seq", link, (ones_heads, zero_state), False
    )
    c_wide = c_blocks.astype(jnp.float32)
    before_block = jnp.concatenate([ones_heads[None], jnp.cumprod(decays, axis=0)[:-1]], axis=0)
    entering = local_enter + before_block[:, :, None, None] * enter_state[None]
    y_state = jnp.exp(cum_decay)[..., None] * jnp.einsum(
        "kqn,khpn->kqhp", c_wide, entering, precision=highest
    )
    y_total = y_intra + y_state + d_skip[:, None] * x_blocks.astype(jnp.float32)
    y_flat = y_total.reshape(tokens_here, heads * HEAD_DIM)
    gated = y_flat * jax.nn.silu(z_local.astype(jnp.float32))
    square_sums = lax.psum(jnp.sum(gated * gated, axis=1), "head")
    normed = (
        gated * lax.rsqrt(square_sums[:, None] / INNER + stability_constant) * norm_gain
    ).astype(jnp.bfloat16)
    last_index = seq_count - 1
    after_decay = prefix(dev_decay, "seq", multiply, ones_heads, True)
    final_state = lax.psum(after_decay[:, None, None] * local_final, "seq")
    keep_x, keep_bc = (broadcast(tail_x, "seq", last_index), broadcast(tail_bc, "seq", last_index))
    slab_index = jnp.sum(
        jnp.where(owner[0] == seq_index, jnp.arange(seq_count, dtype=jnp.int32), 0)
    )
    ssm_state = take_slab(final_state.reshape(heads, -1), slab_index, seq_count)[None, None]
    conv_x_state = take_slab(keep_x, slab_index, seq_count)[None, None]
    conv_bc_state = take_slab(keep_bc, slab_index, seq_count)[None, None]
    features = lax.all_gather(normed, "head", axis=1, tiled=True)
    out_cols = out_weight.shape[1]
    mixed_sum = add_rows(features, lax.all_gather(out_weight, ("seq", "rep"), axis=0, tiled=True))
    mixed = mixed_sum.astype(jnp.bfloat16).reshape(1, tokens_here, out_cols)
    return (mixed, ssm_state, conv_x_state, conv_bc_state)


def solution(mesh):
    return jax.shard_map(
        local,
        mesh=mesh,
        in_specs=(
            P(("grp", "rep"), None, "seq", None, "head"),
            P(("grp", "rep"), None, "seq", None, "head"),
            P(("grp", "rep"), None, "seq", None, None),
            P(("grp", "rep"), None, "seq", None, "head"),
            P("head"),
            P("head"),
            P("head"),
            P(None, "head"),
            P(),
            P("head"),
            P(("seq", "rep"), "head"),
            P(("grp", "rep")),
            P(("grp", "rep"), None),
        ),
        out_specs=(
            P(("grp", "rep"), "seq", "head"),
            P(("grp", "rep"), "seq", "head", None),
            P(("grp", "rep"), "seq", None, "head"),
            P(("grp", "rep"), "seq", None, None),
        ),
        check_vma=False,
    )
```

profile of v0, /device:TPU:0, one launch (start us, length us, event | category | flops | bytes accessed | tf_op | source)
XLA Modules:
  0.0 532.8 jit_solution(8478039113186121479)
XLA Ops:
  7.2 0.7 copy-done
  7.9 0.7 reshape.454
  8.6 6.3 %all-to-all-start.2 = ((bf16[4,2,1024]{2,1,0:T(2,128)(2,1)}), bf16[4,2,1024]{2,1,0:T(2,128)(2,1)S(1)}, u32[]{:S(2)}, u32[]{:S(2)}) async-start(bf16[4,2,1024]{2,1,0:T(2,128)(2,1)} %reshape.454), calls=%async_computation.2 | async-start | bytes 32768 | tf_op jit(solution)/shard_map/all_to_all | solution.py:113
  15.6 1.7 fusion.36
  17.3 1.4 fusion.37
  20.6 4.5 all-to-all-start.1
  25.2 0.7 broadcast_multiply_fusion.1
  26.1 0.7 bitcast_exponential_fusion
  27.1 1.9 copy.80
  29.0 11.5 %all-gather = f32[4,1,64]{2,1,0:T(1,128)S(1)} all-gather(f32[1,1,64]{2,1,0:T(1,128)S(1)} %get-tuple-element.290), channel_id=2, replica_groups=mesh['grp'=2,'seq'=4,'head'=2,'rep'=2] {'seq'}, dimensions={0}, use_global_device_ids=true | all-gather | bytes 1280 | tf_op jit(solution)/shard_map/all_gather | solution.py:25
  40.5 3.7 all-to-all-start
  45.0 0.9 bitcast_select_fusion.1
  46.6 3.8 collective-permute-start.1
  50.4 16.6 %all-to-all-done = bf16[1,4,1,32,4096]{4,3,2,0,1:T(8,128)(2,1)S(1)} async-done(((bf16[1,4,1,32,4096]{4,3,2,0,1:T(8,128)(2,1)}), bf16[1,4,1,32,4096]{4,3,2,0,1:T(8,128)(2,1)S(1)}, u32[]{:S(2)}, u32[]{:S(2)}) %all-to-all-start) | async-done | bytes 1048608 | tf_op jit(solution)/shard_map/all_to_all | solution.py:110
  67.3 1.3 collective-permute-start
  69.2 0.9 multiply_convert_fusion.4
  70.2 3.1 multiply_convert_fusion.2
  73.3 1.6 copy.81
  74.9 2.4 broadcast_multiply_fusion
  77.3 5.7 %all-to-all-start.3 = ((bf16[1,4,1,32,4096]{4,3,2,0,1:T(8,128)(2,1)}), bf16[1,4,1,32,4096]{4,3,2,0,1:T(8,128)(2,1)}, u32[]{:S(2)}, u32[]{:S(2)}) async-start(bf16[1,4,1,32,4096]{4,3,2,0,1:T(8,128)(2,1)} %bitcast.35), calls=%async_computation.3 | async-start | bytes 2097152 | tf_op jit(solution)/shard_map/all_to_all | solution.py:111
  83.5 48.3 %all-to-all-done.3 = bf16[1,4,1,32,4096]{4,3,2,0,1:T(8,128)(2,1)} async-done(((bf16[1,4,1,32,4096]{4,3,2,0,1:T(8,128)(2,1)}), bf16[1,4,1,32,4096]{4,3,2,0,1:T(8,128)(2,1)}, u32[]{:S(2)}, u32[]{:S(2)}) %all-to-all-start.3) | async-done | bytes 1048608 | tf_op jit(solution)/shard_map/all_to_all | solution.py:111
  131.8 2.7 bitcast_convert_fusion
  134.6 4.6 reshape.449
  139.2 4.8 copy.87
  144.0 1.3 copy.72
  145.3 1.7 copy.82
  147.0 3.0 reshape_reshape.3
  150.0 1.1 copy-done.4
  151.2 3.3 fusion.1
  154.4 87.4 %all-gather.10.cloned.1.call-done = f32[256,64,128]{2,1,0:T(8,128)} async-done(((f32[64,64,128]{2,1,0:T(8,128)}), f32[256,64,128]{2,1,0:T(8,128)}) %all-gather.10.cloned.1.call-update) | async-done | bytes 8388624 | tf_op jit(solution)/shard_map/all_gather | solution.py:25
  241.9 11.4 %while.35 = (s32[]{:T(128)}, f32[64,64,128]{2,1,0:T(8,128)S(1)}, s32[]{:T(128)}, f32[4,64]{1,0:T(4,128)}, f32[4,64,64,128]{3,2,1,0:T(8,128)}, /*index=5*/s32[]{:T(128)}, s32[]{:T(128)}) while((s32[]{:T(128)}, f32[64,64,128]{2,1,0:T(8,128)S(1)}, s32[]{:T(128)}, f32[4,64]{1,0:T(4,128)}, f32[4,64,64,128]{3,2,1,0:T(8,128)}, ...), condition=%wide.region_2.3_spmd.clone, body=%wide.region_1.2_spmd.clone.sunk | while | flops 2097156 | bytes 6292329 | solution.py:38
  241.9 0.7 dynamic-slice_bitcast_fusion.4
  242.6 2.1 fusion.44
  244.7 0.7 dynamic-slice_bitcast_fusion.4
  245.3 2.1 fusion.44
  248.1 2.3 fusion.44
  251.1 2.1 fusion.44
  253.2 5.9 %multiply_reduce_fusion = (f32[128]{0:T(128)S(1)}, f32[1,128,64,64]{1,3,2,0:T(8,128)}) fusion(f32[1,128,64,64]{1,3,2,0:T(8,128)} %copy.87, f32[1,128,64,64]{1,3,2,0:T(8,128)} %bitcast.133, f32[64]{0:T(128)S(1)} %copy-done.18, f32[64,64,128]{2,1,0:T(8,128)S(1)} %get-tuple-element.223, bf16[128,256]{1,0:T(8,128)(2,1)S(1)} %multiply_convert_fusion.4, ...), kind=kOutput, calls=%fused_computation.17 | convolution fusion | flops 811073408 | bytes 10552320 | tf_op jit(solution)/shard_map/kqn,khpn->kqhp/dot_general | solution.py:164
  259.1 3.1 copy.85
  262.2 4.9 psum.28
  267.1 3.3 fusion.14
  273.7 18.3 %all-reduce = (bf16[3,4,1024]{2,0,1:T(4,128)(2,1)S(1)}, bf16[3,4,64]{2,0,1:T(4,128)(2,1)S(1)}) all-reduce(bf16[3,4,1024]{2,0,1:T(4,128)(2,1)S(1)} %bitcast.140, bf16[3,4,64]{2,0,1:T(4,128)(2,1)S(1)} %copy.89), channel_id=1, replica_groups=mesh['grp'=2,'seq'=4,'head'=2,'rep'=2] {'seq'}, use_global_device_ids=true, to_apply=%region_9.10 | all-reduce | flops 13056 | bytes 52224 | tf_op jit(solution)/shard_map/psum | solution.py:43
  293.2 37.3 %all-reduce.3.cloned.1.call-done = f32[64,4,2048]{2,1,0:T(4,128)} async-done(((f32[64,4,2048]{2,1,0:T(4,128)}), f32[64,4,2048]{2,1,0:T(4,128)}) %all-reduce.3.cloned.1.call-update) | async-done | bytes 2097168 | tf_op jit(solution)/shard_map/psum | solution.py:176
  330.5 2.1 constant_dynamic-slice_fusion
  332.7 1.0 copy.92
  333.6 30.6 %all-gather.6.cloned.1.call-done = bf16[128,8192]{1,0:T(8,128)(2,1)} async-done(((bf16[128,4096]{1,0:T(8,128)(2,1)}), bf16[128,8192]{1,0:T(8,128)(2,1)}) %all-gather.6.cloned.1.call-update) | async-done | bytes 2097168 | tf_op jit(solution)/shard_map/all_gather | solution.py:184
  364.2 152.6 %all-gather.8.cloned.1.call-done = bf16[8192,1024]{1,0:T(8,128)(2,1)} async-done(((bf16[1024,1024]{1,0:T(8,128)(2,1)}), bf16[8192,1024]{1,0:T(8,128)(2,1)}) %all-gather.8.cloned.1.call-update) | async-done | bytes 16777232 | tf_op jit(solution)/shard_map/all_gather | solution.py:186
  516.8 9.5 %fusion.16 = bf16[1,128,1024]{2,1,0:T(8,128)(2,1)} fusion(bf16[128,8192]{1,0:T(8,128)(2,1)} %all-gather.6.cloned.1.call-done, bf16[8192,1024]{1,0:T(8,128)(2,1)} %all-gather.8.cloned.1.call-done), kind=kOutput, calls=%fused_computation.31 | convolution fusion | flops 2147614720 | bytes 19136512 | tf_op jit(solution)/shard_map/dot_general | solution.py:86
  (83 shorter events, 9.2 us)
Async XLA Ops:
  7.2 0.8 copy-start
  8.6 12.0 %all-to-all-start.2 = ((bf16[4,2,1024]{2,1,0:T(2,128)(2,1)}), bf16[4,2,1024]{2,1,0:T(2,128)(2,1)S(1)}, u32[]{:S(2)}, u32[]{:S(2)}) async-start(bf16[4,2,1024]{2,1,0:T(2,128)(2,1)} %reshape.454), calls=%async_computation.2 | async-start | bytes 32768 | tf_op jit(solution)/shard_map/all_to_all | solution.py:113
  19.3 7.5 %copy-start.11 = (f32[128]{0:T(128)}, f32[128]{0:T(128)S(1)}, u32[]{:S(2)}) copy-start(f32[128]{0:T(128)S(1)} %get-tuple-element.282) | copy-start | bytes 1540
  20.6 19.9 %all-to-all-start.1 = ((bf16[1,4,1,32,256]{4,3,2,0,1:T(8,128)(2,1)}), bf16[1,4,1,32,256]{4,3,2,0,1:T(8,128)(2,1)S(1)}, u32[]{:S(2)}, u32[]{:S(2)}) async-start(bf16[1,4,1,32,256]{4,3,2,0,1:T(8,128)(2,1)} %bitcast.145), calls=%async_computation.1 | async-start | bytes 131072 | tf_op jit(solution)/shard_map/all_to_all | solution.py:112
  29.0 15.8 %copy-start.6 = (f32[64]{0:T(128)S(1)}, f32[64]{0:T(128)}, u32[]{:S(2)}) copy-start(f32[64]{0:T(128)} %custom-call.1) | copy-start | bytes 772
  29.0 16.0 %copy-start.15 = (pred[128]{0:T(512)(128)(4,1)S(1)}, pred[128]{0:T(512)(128)(4,1)}, u32[]{:S(2)}) copy-start(pred[128]{0:T(512)(128)(4,1)} %get-tuple-element.283) | copy-start | bytes 388
  40.5 4.5 copy-start.5
  40.5 29.6 %copy-start.3 = (f32[128,4096]{1,0:T(8,128)S(1)}, f32[128,4096]{1,0:T(8,128)}, u32[]{:S(2)}) copy-start(f32[128,4096]{1,0:T(8,128)} %copy.80) | copy-start | bytes 6291460
  40.5 26.5 %all-to-all-start = ((bf16[1,4,1,32,4096]{4,3,2,0,1:T(8,128)(2,1)}), bf16[1,4,1,32,4096]{4,3,2,0,1:T(8,128)(2,1)S(1)}, u32[]{:S(2)}, u32[]{:S(2)}) async-start(bf16[1,4,1,32,4096]{4,3,2,0,1:T(8,128)(2,1)} %bitcast.135), calls=%async_computation | async-start | bytes 2097152 | tf_op jit(solution)/shard_map/all_to_all | solution.py:110
  44.2 197.7 %all-gather.10.cloned.1.call-start = ((), (), s32[]{:S(2)}) async-start(), calls=%async_computation.7 | async-start | bytes 10485760 | tf_op jit(solution)/shard_map/all_gather | solution.py:25
  45.0 22.0 %copy-start.7 = (f32[64]{0:T(128)}, f32[64]{0:T(128)S(1)}, u32[]{:S(2)}) copy-start(f32[64]{0:T(128)S(1)} %get-tuple-element.224) | copy-start | bytes 772
  45.0 22.0 %copy-start.10 = (f32[4,64]{1,0:T(4,128)}, f32[4,64]{1,0:T(4,128)S(1)}, u32[]{:S(2)}) copy-start(f32[4,64]{1,0:T(4,128)S(1)} %get-tuple-element.430) | copy-start | bytes 3076
  46.6 22.0 %collective-permute-start.1 = (bf16[3,256]{1,0:T(4,128)(2,1)S(1)}, bf16[3,256]{1,0:T(4,128)(2,1)S(1)}, u32[]{:S(2)}, u32[]{:S(2)}) collective-permute-start(bf16[3,256]{1,0:T(4,128)(2,1)S(1)} %get-tuple-element.287), channel_id=1, source_target_pairs={{0,4},{4,8},{8,12},{1,5},{5,9},{9,13},{2,6},{6,10},{10,14},{3,7},{... | collective-permute-start | bytes 4616 | tf_op jit(solution)/shard_map/ppermute | solution.py:20
  67.3 2.9 collective-permute-start
  68.6 0.6 copy-start.16
  73.3 1.6 copy-start.8
  73.3 1.6 copy-start.17
  77.3 5.7 %copy-start.12 = (f32[128]{0:T(128)S(1)}, f32[128]{0:T(128)}, u32[]{:S(2)}) copy-start(f32[128]{0:T(128)} %copy-done.11) | copy-start | bytes 1540
  77.3 5.8 %copy-start.14 = (f32[64]{0:T(128)S(1)}, f32[64]{0:T(128)}, u32[]{:S(2)}) copy-start(f32[64]{0:T(128)} %param.22) | copy-start | bytes 772
  77.3 54.5 %all-to-all-start.3 = ((bf16[1,4,1,32,4096]{4,3,2,0,1:T(8,128)(2,1)}), bf16[1,4,1,32,4096]{4,3,2,0,1:T(8,128)(2,1)}, u32[]{:S(2)}, u32[]{:S(2)}) async-start(bf16[1,4,1,32,4096]{4,3,2,0,1:T(8,128)(2,1)} %bitcast.35), calls=%async_computation.3 | async-start | bytes 2097152 | tf_op jit(solution)/shard_map/all_to_all | solution.py:111
  83.0 247.5 %all-reduce.3.cloned.1.call-start = ((), (), s32[]{:S(2)}) async-start(), calls=%async_computation.6 | async-start | bytes 4194304 | tf_op jit(solution)/shard_map/psum | solution.py:176
  149.9 1.2 copy-start.4
  150.0 214.3 %all-gather.6.cloned.1.call-start = ((), (), s32[]{:S(2)}) async-start(), calls=%async_computation.4 | async-start | bytes 3145728 | tf_op jit(solution)/shard_map/all_gather | solution.py:184
  241.9 11.4 %copy-start.18 = (f32[64]{0:T(128)S(1)}, f32[64]{0:T(128)}, u32[]{:S(2)}) copy-start(f32[64]{0:T(128)} %param.23) | copy-start | bytes 772
  259.1 8.0 %copy-start.2 = (f32[1,4,1,32,4096]{4,3,1,2,0:T(8,128)S(1)}, f32[1,4,1,32,4096]{4,3,1,2,0:T(8,128)}, u32[]{:S(2)}) copy-start(f32[1,4,1,32,4096]{4,3,1,2,0:T(8,128)} %bitcast_convert_fusion) | copy-start | bytes 6291460
  259.1 8.0 %copy-start.9 = (f32[4096]{0:T(1024)S(1)}, f32[4096]{0:T(1024)}, u32[]{:S(2)}) copy-start(f32[4096]{0:T(1024)} %param.26) | copy-start | bytes 49156
  270.4 0.7 copy-start.19
  270.4 3.2 copy-start.13
  270.4 246.4 %all-gather.8.cloned.1.call-start = ((), (), s32[]{:S(2)}) async-start(), calls=%async_computation.5 | async-start | bytes 18874368 | tf_op jit(solution)/shard_map/all_gather | solution.py:186
  516.8 9.5 %copy-start.1 = (bf16[1,4,1,32,64]{4,3,2,1,0:T(8,128)(2,1)S(1)}, bf16[1,4,1,32,64]{4,3,2,1,0:T(8,128)(2,1)}, u32[]{:S(2)}) copy-start(bf16[1,4,1,32,64]{4,3,2,1,0:T(8,128)(2,1)} %param.20) | copy-start | bytes 49156
Sparse Core Ops, SparseCore 0:
  77.4 164.3 all-gather.9
  244.2 86.2 all-reduce.2
  332.1 32.1 all-gather.5
  365.7 151.0 all-gather.7
where the time goes:
time: 534 us; the launch traced here: 533 us
  waiting for transfers between devices  374 us (70%)
  local copies, waits for them, and re-layouts  36.1 us (7%)
  blocking collectives  34.7 us (6%)
  starting transfers between devices  25.4 us (5%)
  other arithmetic  24.6 us (5%)
  matrix products  21.1 us (4%)
  between operations  16.6 us (3%)
    all_gather x1, waiting for transfers between devices, local(): lax.all_gather(out_weight, ('seq', 'rep'), axis=0, tiled=True)  153 us
    all_gather x1, waiting for transfers between devices, prefix(): everything = jax.tree.map(lambda part: lax.all_gather(part, axis), value)  87.4 us
    all_to_all x1, waiting for transfers between devices, local(): lax.all_to_all(gate_proj, 'seq', split_axis=1, concat_axis=2, tiled=True)  48.3 us
    psum x1, waiting for transfers between devices, local(): final_state = lax.psum(after_decay[:, None, None] * local_final, 'seq')  37.3 us
    all_gather x1, waiting for transfers between devices, local(): features = lax.all_gather(normed, 'head', axis=1, tiled=True)  30.6 us
    psum x1, blocking collectives, broadcast(): return lax.psum(block, axis)  18.3 us
    all_to_all x1, waiting for transfers between devices, local(): lax.all_to_all(x_proj, 'seq', split_axis=1, concat_axis=2, tiled=True)  16.6 us
    all_gather x1, blocking collectives, prefix(): everything = jax.tree.map(lambda part: lax.all_gather(part, axis), value)  11.5 us
  transfers between devices with their start and end apart: 10, of which 8 were waited for; matrix products, arithmetic and copies ran while one was open for 12% of the time, Pallas kernels for 0%

commit v1 on v0

--- a/solution.py
+++ b/solution.py
@@ -1,6 +1,10 @@
+import functools
+
 import jax
 import jax.numpy as jnp
 from jax import lax
+from jax.experimental import pallas as pl
+from jax.experimental.pallas import tpu as pltpu
 from jax.sharding import PartitionSpec as P
 
 HEAD_DIM = 64
@@ -188,9 +192,424 @@
     return (mixed, ssm_state, conv_x_state, conv_bc_state)
 
 
+MESH = pl.DeviceIdType.MESH
+LANES = 128
+PAD = 8
+F32 = jnp.float32
+BF16 = jnp.bfloat16
+NT = (((1,), (1,)), ((), ()))
+TN = (((0,), (0,)), ((), ()))
+
+
+def split3(value):
+    hi = value.astype(BF16)
+    rest = value - hi.astype(F32)
+    mid = rest.astype(BF16)
+    return hi, mid, (rest - mid.astype(F32)).astype(BF16)
+
+
+def pick(parts, chosen):
+    return sum(jnp.dot(parts[k], chosen, preferred_element_type=F32) for k in range(3))
+
+
+def silu(value):
+    return value * (1.0 / (1.0 + jnp.exp(-value)))
+
+
+def fused_kernel(
+    sizes,
+    start_ref, owner_ref, x_ref, z_ref, bc_ref, dt_ref, rate_ref, bias_ref, skip_ref,
+    cw_ref, cbw_ref, gain_ref, w_ref,
+    mixed_ref, ssm_ref, tailx_ref, tailbc_ref,
+    xs, zs, bcs, dts, xpad, bpad, b_scr, c_scr, cum3, step3, rows_t, scores, y_scr, g_scr,
+    fin, fsnd, frecv, tails, wfull, psnd, precv, pown, qsnd, qrecv, ssnd, srecv,
+    sx, rx, sz, rz, sb, rb, sd, rd, sw, rw, swf, rwf, st, rt, sf, rf, sp, rp, sq, rq, ss, rs,
+):
+    n_grp, n, n_head, n_rep = (sizes[a] for a in ("grp", "seq", "head", "rep"))
+    me, head = lax.axis_index("seq"), lax.axis_index("head")
+    grp, rep = lax.axis_index("grp"), lax.axis_index("rep")
+    nb, _, sub, width = xs.shape
+    length = nb * n * sub
+    blocks = length // SPAN
+    heads = dt_ref.shape[2]
+    own_heads = heads // n
+    out_cols = w_ref.shape[1]
+
+    def exchange(src_of, dst_of, send, recv):
+        copies = []
+        for o in range(1, n):
+            to = lax.rem(me + o, n)
+            copies.append(pltpu.make_async_remote_copy(
+                src_ref=src_of(to), dst_ref=dst_of, send_sem=send.at[o], recv_sem=recv.at[o],
+                device_id={"seq": to}, device_id_type=MESH))
+        own = pltpu.make_async_copy(src_of(me), dst_of, recv.at[0])
+        for copy in copies:
+            copy.start()
+        own.start()
+        return copies + [own]
+
+    def cols(j):
+        return pl.ds(pl.multiple_of(j * width, LANES), width)
+
+    bc_copies = exchange(lambda j: bc_ref, bcs.at[:, me], sb, rb)
+    dt_copies = exchange(lambda j: dt_ref, dts.at[:, me], sd, rd)
+    x_copies = exchange(lambda j: x_ref.at[:, :, cols(j)], xs.at[:, me], sx, rx)
+    z_copies = exchange(lambda j: z_ref.at[:, :, cols(j)], zs.at[:, me], sz, rz)
+
+    w_rows = w_ref.shape[0] // n_grp
+    part = me * n_rep + rep
+    to_seq, to_head, to_rep = lax.rem(part, n), part // n, head
+    w_self = (to_seq == me) & (to_head == head) & (to_rep == rep)
+
+    def w_piece(g, c):
+        return wfull.at[pl.ds(pl.multiple_of(g * w_rows, 16), w_rows),
+                        pl.ds(pl.multiple_of(c * out_cols, LANES), out_cols)]
+
+    w_src = w_ref.at[pl.ds(pl.multiple_of(grp * w_rows, 16), w_rows), :]
+    w_copy = pltpu.make_async_remote_copy(
+        src_ref=w_src, dst_ref=w_piece(grp, head), send_sem=sw, recv_sem=rw,
+        device_id={"seq": to_seq, "head": to_head, "rep": to_rep}, device_id_type=MESH)
+
+    @pl.when(w_self)
+    def _():
+        pltpu.make_async_copy(w_src, w_piece(grp, head), rw).start()
+
+    @pl.when(jnp.logical_not(w_self))
+    def _():
+        w_copy.start()
+
+    begin = start_ref[0]
+    live = lax.broadcasted_iota(jnp.int32, (length, LANES), 0) >= begin
+    row_id = lax.broadcasted_iota(jnp.int32, (SPAN, SPAN), 0)
+    col_id = lax.broadcasted_iota(jnp.int32, (SPAN, SPAN), 1)
+    causal = row_id >= col_id
+    head_row = lax.broadcasted_iota(jnp.int32, (heads, LANES), 0)
+    lane_head = lax.broadcasted_iota(jnp.int32, (heads, LANES), 1) // HEAD_DIM
+    per_chunk = LANES // HEAD_DIM
+
+    for copy in bc_copies + dt_copies:
+        copy.wait()
+
+    bpad[0:PAD, :] = jnp.zeros((PAD, bpad.shape[1]), F32)
+    xpad[0:PAD, :] = jnp.zeros((PAD, LANES), F32)
+    for half, target in ((0, b_scr), (1, c_scr)):
+        at = pl.ds(half * NSTATE, NSTATE)
+        bv = bcs[:, :, :, at].reshape(length, NSTATE).astype(F32)
+        bpad[PAD:, at] = jnp.where(live, bv, 0.0)
+        acc = jnp.zeros((length, NSTATE), F32)
+        for k in range(KCONV):
+            acc = acc + cbw_ref[k : k + 1, at] * bpad[pl.ds(PAD - KCONV + 1 + k, length), at]
+        target[...] = silu(acc).astype(BF16)
+
+    d = dts[...].reshape(length, heads).astype(F32) + bias_ref[...]
+    step = jnp.maximum(d, 0.0) + jnp.log1p(jnp.exp(-jnp.abs(d)))
+    step = jnp.where(live[:, :heads], step, 0.0)
+    decay = -rate_ref[...] * step
+    lower = causal.astype(F32)
+    eye = (lax.broadcasted_iota(jnp.int32, (heads, heads), 0)
+           == lax.broadcasted_iota(jnp.int32, (heads, heads), 1)).astype(F32)
+    for c in range(blocks):
+        r = slice(c * SPAN, (c + 1) * SPAN)
+        cum = jnp.dot(lower, decay[r], precision=highest, preferred_element_type=F32)
+        for k, (a, b) in enumerate(zip(split3(cum), split3(step[r]))):
+            cum3[k, r, :] = a
+            step3[k, r, :] = b
+        rows_t[0, c] = lax.dot_general(eye, cum, NT, precision=highest, preferred_element_type=F32)
+        rows_t[1, c] = lax.dot_general(eye, step[r], NT, precision=highest, preferred_element_type=F32)
+        raw = lax.dot_general(c_scr[r, :], b_scr[r, :], NT, preferred_element_type=F32)
+        scores[c] = jnp.where(causal, raw, 0.0)
+
+    for copy in x_copies:
+        copy.wait()
+    tail_src = xs.at[nb - 1, n - 1, sub - 16 : sub, :]
+    t_copies = exchange(lambda j: tail_src, tails.at[me], st, rt)
+
+    left = lax.broadcasted_iota(jnp.int32, (SPAN, LANES), 1) < HEAD_DIM
+
+    @pl.loop(0, width // LANES)
+    def _(i):
+        lanes = pl.ds(pl.multiple_of(i * LANES, LANES), LANES)
+        wide = pl.ds(pl.multiple_of(me * width + i * LANES, LANES), LANES)
+        xv = xs[:, :, :, lanes].reshape(length, LANES).astype(F32)
+        xpad[PAD:, :] = jnp.where(live, xv, 0.0)
+        acc = jnp.zeros((length, LANES), F32)
+        for k in range(KCONV):
+            acc = acc + cw_ref[k : k + 1, wide] * xpad[pl.ds(PAD - KCONV + 1 + k, length), :]
+        xc = silu(acc).astype(BF16)
+        first = me * own_heads + i * per_chunk
+        chosen_f = (head_row == first + lane_head).astype(F32)
+        chosen = chosen_f.astype(BF16)
+        cum_l = pick(cum3, chosen)
+        step_l = pick(step3, chosen)
+        skip = jnp.dot(jnp.broadcast_to(skip_ref[...], (8, heads)), chosen_f, precision=highest,
+                       preferred_element_type=F32)[0:1]
+        state = jnp.zeros((NSTATE, LANES), F32)
+        for c in range(blocks):
+            r = slice(c * SPAN, (c + 1) * SPAN)
+            cl, sl, xb = cum_l[r], step_l[r], xc[r]
+            y = skip * xb.astype(F32)
+            for k in range(per_chunk):
+                cum_q = jnp.broadcast_to(cl[:, k * HEAD_DIM : k * HEAD_DIM + 1], (SPAN, SPAN))
+                cum_t = rows_t[0, c, pl.ds(first + k, 1), :]
+                step_t = rows_t[1, c, pl.ds(first + k, 1), :]
+                mix = (scores[c] * jnp.exp(jnp.minimum(cum_q - cum_t, 0.0)) * step_t).astype(BF16)
+                xk = jnp.where(left if k == 0 else jnp.logical_not(left), xb.astype(F32), 0.0).astype(BF16)
+                y = y + jnp.dot(mix, xk, preferred_element_type=F32)
+            if c:
+                y = y + jnp.exp(cl) * jnp.dot(c_scr[r, :], state.astype(BF16), preferred_element_type=F32)
+            y_scr[r, lanes] = y
+            last = cl[SPAN - 1 : SPAN, :]
+            scaled = (jnp.exp(last - cl) * sl * xb.astype(F32)).astype(BF16)
+            state = jnp.exp(last) * state + lax.dot_general(
+                b_scr[r, :], scaled, TN, preferred_element_type=F32)
+        fin[pl.ds(i * per_chunk, per_chunk)] = state.T.reshape(per_chunk, n, HEAD_DIM // n, NSTATE)
+
+    def slab_of(s):
+        return jnp.minimum(sum(jnp.where(owner_ref[j] == s, j, 0) for j in range(n)), n - 1)
+
+    f_copies = []
+    for o in range(1, n):
+        to = lax.rem(me + o, n)
+        fsnd[o] = fin[:, slab_of(to)]
+        f_copies.append(pltpu.make_async_remote_copy(
+            src_ref=fsnd.at[o], dst_ref=frecv.at[me], send_sem=sf.at[o], recv_sem=rf.at[o],
+            device_id={"seq": to}, device_id_type=MESH))
+
+    for copy in z_copies:
+        copy.wait()
+
+    def gate_chunk(i, total):
+        lanes = pl.ds(pl.multiple_of(i * LANES, LANES), LANES)
+        wide = pl.ds(pl.multiple_of(me * width + i * LANES, LANES), LANES)
+        zv = zs[:, :, :, lanes].reshape(length, LANES).astype(F32)
+        gated = y_scr[:, lanes] * silu(zv)
+        g_scr[:, lanes] = (gated * gain_ref[:, wide]).astype(BF16)
+        return total + gated * gated
+
+    squares = lax.fori_loop(0, width // LANES, gate_chunk, jnp.zeros((length, LANES), F32))
+    for c in range(blocks):
+        r = slice(c * SPAN, (c + 1) * SPAN)
+        total = jnp.broadcast_to(jnp.sum(squares[r], axis=1, keepdims=True), (SPAN, LANES))
+        ssnd[c] = total.T[0:8, :]
+
+    @pl.when(w_self)
+    def _():
+        pltpu.make_async_copy(w_src, w_piece(grp, head), rw).wait()
+
+    @pl.when(jnp.logical_not(w_self))
+    def _():
+        w_copy.wait()
+
+    wf_copies = []
+    for og in range(n_grp):
+        for orr in range(n_rep):
+            if og or orr:
+                slot = og * n_rep + orr
+                wf_copies.append(pltpu.make_async_remote_copy(
+                    src_ref=w_piece(grp, rep), dst_ref=w_piece(grp, rep),
+                    send_sem=swf.at[slot], recv_sem=rwf.at[slot],
+                    device_id={"grp": lax.rem(grp + og, n_grp), "rep": lax.rem(rep + orr, n_rep)},
+                    device_id_type=MESH))
+    for copy in wf_copies:
+        copy.start()
+
+    s_copies = []
+    for oh in range(n_head):
+        for o in range(n):
+            if oh or o:
+                to = lax.rem(me + o, n)
+                slot = oh * n + o
+                s_copies.append(pltpu.make_async_remote_copy(
+                    src_ref=ssnd.at[to], dst_ref=srecv.at[slot], send_sem=ss.at[slot],
+                    recv_sem=rs.at[slot],
+                    device_id={"seq": to, "head": lax.rem(head + oh, n_head)}, device_id_type=MESH))
+    for copy in s_copies + f_copies:
+        copy.start()
+    for copy in wf_copies:
+        copy.wait()
+
+    tile = 256 if out_cols % 256 == 0 else LANES
+
+    def product(h, put):
+        @pl.loop(0, out_cols // tile)
+        def _(i):
+            at = pl.ds(pl.multiple_of(h * out_cols + i * tile, LANES), tile)
+            out = jnp.dot(g_scr[...], wfull[:, at], preferred_element_type=F32)
+            put(pl.ds(pl.multiple_of(i * tile, LANES), tile), out.reshape(blocks, SPAN, tile))
+
+    p_copies = {}
+    for oh in range(1, n_head):
+        to_h = lax.rem(head + oh, n_head)
+
+        def put(at, out, oh=oh):
+            psnd[oh - 1, :, :, at] = out.astype(BF16)
+
+        product(to_h, put)
+        for o in [*range(1, n), 0]:
+            block = lax.rem(me + o, n)
+            p_copies[oh, o] = pltpu.make_async_remote_copy(
+                src_ref=psnd.at[oh - 1, block], dst_ref=precv.at[oh - 1, block],
+                send_sem=sp.at[oh - 1, o], recv_sem=rp.at[oh - 1, o],
+                device_id={"head": to_h}, device_id_type=MESH)
+            p_copies[oh, o].start()
+
+    def put_own(at, out):
+        pown[:, :, at] = out
+
+    product(head, put_own)
+
+    q_copies = []
+    for o in [*range(1, n), 0]:
+        block = lax.rem(me + o, n)
+        whole = pown[block]
+        for oh in range(1, n_head):
+            p_copies[oh, o].wait()
+            whole = whole + precv[oh - 1, block].astype(F32)
+        if o:
+            qsnd[o] = whole.astype(BF16)
+            q_copies.append(pltpu.make_async_remote_copy(
+                src_ref=qsnd.at[o], dst_ref=qrecv.at[o], send_sem=sq.at[o], recv_sem=rq.at[o],
+                device_id={"seq": block}, device_id_type=MESH))
+            q_copies[-1].start()
+        else:
+            pown[block] = whole
+
+    for copy in s_copies + t_copies:
+        copy.wait()
+    total = ssnd[me]
+    for slot in range(1, n * n_head):
+        total = total + srecv[slot]
+    scale_row = lax.rsqrt(total / INNER + stability_constant)
+    scale = jnp.broadcast_to(scale_row[0:1], (SPAN, LANES)).T
+
+    slab = slab_of(me)
+    tail_live = length - 16 + lax.broadcasted_iota(jnp.int32, (16, width), 0) >= begin
+    tailx_ref[...] = jnp.where(tail_live, tails[slab].astype(F32), 0.0).astype(BF16)
+    state_cols = tailbc_ref.shape[1]
+    wide_bc = bcs.shape[3]
+    chosen = (lax.broadcasted_iota(jnp.int32, (wide_bc, state_cols), 0)
+              == slab * state_cols + lax.broadcasted_iota(jnp.int32, (wide_bc, state_cols), 1)).astype(BF16)
+    tailbc_ref[...] = jnp.dot(
+        bpad[PAD + length - 16 : PAD + length, :].astype(BF16), chosen, preferred_element_type=F32).astype(BF16)
+
+    for copy in f_copies:
+        copy.wait()
+    frecv[me] = fin[:, slab]
+    ssm_ref[...] = frecv[...]
+
+    for copy in q_copies:
+        copy.wait()
+    for at in range(0, out_cols, LANES):
+        lanes = slice(at, at + LANES)
+        whole = pown[me, :, lanes]
+        for o in range(1, n):
+            whole = whole + qrecv[o, :, lanes].astype(F32)
+        mixed_ref[:, lanes] = (whole * scale).astype(BF16)
+
+
+def fused(
+    sizes, x_proj, gate_proj, bc_proj, dt_proj, a_rate, dt_bias, d_skip, conv_x_weight,
+    conv_bc_weight, norm_gain, out_weight, request_first_position, owner,
+):
+    n_grp, n, n_head, n_rep = (sizes[a] for a in ("grp", "seq", "head", "rep"))
+    nb, sub, channels = x_proj.shape[1], x_proj.shape[3], x_proj.shape[4]
+    heads, bc_cols = dt_proj.shape[4], bc_proj.shape[4]
+    length, width = nb * n * sub, channels // n
+    blocks, own_heads, out_cols = length // SPAN, heads // n, out_weight.shape[1]
+    piece = HEAD_DIM // n
+    vmem = lambda shape, kind: pltpu.VMEM(shape, kind)
+    dma = lambda *shape: pltpu.SemaphoreType.DMA(shape)
+    hbm = pl.BlockSpec(memory_space=pl.ANY)
+    here = pl.BlockSpec(memory_space=pltpu.VMEM)
+    smem = pl.BlockSpec(memory_space=pltpu.SMEM)
+    mixed, ssm, tail_x, tail_bc = pl.pallas_call(
+        functools.partial(fused_kernel, sizes),
+        out_shape=(
+            jax.ShapeDtypeStruct((SPAN, out_cols), BF16),
+            jax.ShapeDtypeStruct((n, own_heads, piece, NSTATE), F32),
+            jax.ShapeDtypeStruct((16, width), BF16),
+            jax.ShapeDtypeStruct((16, bc_cols // n), BF16),
+        ),
+        in_specs=[smem, smem, hbm, hbm, hbm, hbm] + [here] * 6 + [hbm],
+        out_specs=(here,) * 4,
+        scratch_shapes=[
+            vmem((nb, n, sub, width), BF16),
+            vmem((nb, n, sub, width), BF16),
+            vmem((nb, n, sub, bc_cols), BF16),
+            vmem((nb, n, sub, heads), BF16),
+            vmem((length + PAD, LANES), F32),
+            vmem((length + PAD, bc_cols), F32),
+            vmem((length, NSTATE), BF16),
+            vmem((length, NSTATE), BF16),
+            vmem((3, length, heads), BF16),
+            vmem((3, length, heads), BF16),
+            vmem((2, blocks, heads, SPAN), F32),
+            vmem((blocks, SPAN, SPAN), F32),
+            vmem((length, width), F32),
+            vmem((length, width), BF16),
+            vmem((own_heads, n, piece, NSTATE), F32),
+            vmem((n, own_heads, piece, NSTATE), F32),
+            vmem((n, own_heads, piece, NSTATE), F32),
+            vmem((n, 16, width), BF16),
+            vmem((width, out_cols * n_head), BF16),
+            vmem((n_head - 1, blocks, SPAN, out_cols), BF16),
+            vmem((n_head - 1, blocks, SPAN, out_cols), BF16),
+            vmem((blocks, SPAN, out_cols), F32),
+            vmem((n, SPAN, out_cols), BF16),
+            vmem((n, SPAN, out_cols), BF16),
+            vmem((blocks, 8, LANES), F32),
+            vmem((n * n_head, 8, LANES), F32),
+            dma(n), dma(n), dma(n), dma(n), dma(n), dma(n), dma(n), dma(n),
+            pltpu.SemaphoreType.DMA, pltpu.SemaphoreType.DMA,
+            dma(n_grp * n_rep), dma(n_grp * n_rep),
+            dma(n), dma(n), dma(n), dma(n),
+            dma(n_head - 1, n), dma(n_head - 1, n),
+            dma(n), dma(n), dma(n * n_head), dma(n * n_head),
+        ],
+        compiler_params=pltpu.CompilerParams(
+            has_side_effects=True, vmem_limit_bytes=56 * 1024 * 1024
+        ),
+    )(
+        request_first_position,
+        owner.reshape(n),
+        x_proj.reshape(nb, sub, channels),
+        gate_proj.reshape(nb, sub, channels),
+        bc_proj.reshape(nb, sub, bc_cols),
+        dt_proj.reshape(nb, sub, heads),
+        a_rate[None],
+        dt_bias[None],
+        d_skip[None],
+        conv_x_weight,
+        conv_bc_weight,
+        norm_gain[None],
+        out_weight,
+    )
+    rim = KCONV - 1
+    return (
+        mixed[None],
+        ssm.reshape(1, 1, heads, piece * NSTATE),
+        tail_x[16 - rim :][None, None],
+        tail_bc[16 - rim :][None, None],
+    )
+
+
+def either(sizes, x_proj, *rest):
+    n, n_head, n_rep = sizes["seq"], sizes["head"], sizes["rep"]
+    nb, sub, channels = x_proj.shape[1], x_proj.shape[3], x_proj.shape[4]
+    fits = (
+        nb * sub == SPAN
+        and nb == n
+        and sub % 16 == 0
+        and n_head == n_rep
+        and channels % (n * LANES) == 0
+        and rest[9].shape[0] * n == channels
+    )
+    return fused(sizes, x_proj, *rest) if fits else local(x_proj, *rest)
+
+
 def solution(mesh):
     return jax.shard_map(
-        local,
+        functools.partial(either, dict(mesh.shape)),
         mesh=mesh,
         in_specs=(
             P(("grp", "rep"), None, "seq", None, "head"),

time: 534 us -> 179 us (0.34)
  waiting for transfers between devices: 374 us -> 0 us
  Pallas kernels: 0 us -> 169 us
  blocking collectives: 34.7 us -> 0 us
  local copies, waits for them, and re-layouts: 36.1 us -> 6.15 us
  starting transfers between devices: 25.4 us -> 0 us
  other arithmetic: 24.6 us -> 0 us
  matrix products: 21.1 us -> 0 us
  between operations: 16.6 us -> 1.29 us
    all_gather x3 -> x0, waiting for transfers between devices: 271 us -> none  [the longest x1 153 us: local(): lax.all_gather(out_weight, ('seq', 'rep'), axis=0, tiled=True)]
    pallas_call x0 -> x1, Pallas kernels: none -> 169 us  [fused(): pl.pallas_call(functools.partial(fused_kernel, sizes), out_shape=(jax.Sha...]
    all_to_all x4 -> x0, waiting for transfers between devices: 65.6 us -> none  [the longest x1 48.3 us: local(): lax.all_to_all(gate_proj, 'seq', split_axis=1, concat_axis=2, tiled=True)]
    psum x1 -> x0, waiting for transfers between devices: 37.3 us -> none  [local(): final_state = lax.psum(after_decay[:, None, None] * local_final, 'seq')]
    psum x2 -> x0, blocking collectives: 23.2 us -> none  [the longest x1 18.3 us: broadcast(): return lax.psum(block, axis)]
    dot_general x5 -> x0, matrix products: 21.1 us -> none  [the longest x1 9.45 us: add_rows(): return jnp.dot(source, piece, preferred_element_type=jnp.float32)]
    all_to_all x4 -> x0, starting transfers between devices: 20.2 us -> none  [the longest x1 6.35 us: local(): lax.all_to_all(dt_proj, 'seq', split_axis=1, concat_axis=2, tiled=True)]
    convert_element_type x5 -> x0, local copies, waits for them, and re-layouts: 14 us -> none  [the longest x2 9.42 us: local(): gated = y_flat * jax.nn.silu(z_local.astype(jnp.float32))]
  transfers between devices with their start and end apart: 10 -> 0, of which waited for: 8 -> 0; matrix products, arithmetic and copies ran while one was open for 12% -> 0% of each run, Pallas kernels for 0% -> 0%
where the time goes in v1:
time: 179 us; the launch traced here: 177 us
  Pallas kernels  169 us (94%)
  local copies, waits for them, and re-layouts  6.15 us (3%)
    pallas_call x1, Pallas kernels, fused(): pl.pallas_call(functools.partial(fused_kernel, sizes), out_shape=(jax.Sha...  169 us

profile of v1, /device:TPU:0, one launch (start us, length us, event | category | flops | bytes accessed | tf_op | source)
XLA Modules:
  0.0 176.9 jit_solution(18117519294443223457)
XLA Ops:
  1.3 169.5 %shard_map.156 = (bf16[128,1024]{1,0:T(8,128)(2,1)}, f32[4,16,16,128]{3,2,1,0:T(8,128)}, bf16[16,1024]{1,0:T(8,128)(2,1)}, bf16[16,64]{1,0:T(8,128)(2,1)}) custom-call(s32[1]{0:T(128)S(6)} %copy.18.start_ref, s32[4]{0:T(128)} %bitcast.22, bf16[4,32,4096]{2,1,0:T(8,128)(2,1)} %bitcast.16, bf16[4,32,4096]{2,1,0:T(8,128)(2,1)} %bitcast.17, ...), custom_call_target="tpu_custom_call" | custom-call | tf_op jit(solution)/shard_map/pallas_call | solution.py:525
  170.7 1.2 slice_bitcast_fusion.1
  172.0 1.3 slice_bitcast_fusion
  173.3 1.9 %reshape.31 = f32[1,1,64,2048]{3,2,1,0:T(8,128)} reshape(f32[4,16,16,128]{3,2,1,0:T(8,128)} %get-tuple-element.9) | data formatting | bytes 1048576 | tf_op jit(solution)/shard_map/reshape | solution.py:590
  175.2 1.7 copy.19

commit v2 on v1

--- a/solution.py
+++ b/solution.py
@@ -253,8 +253,6 @@
 
     bc_copies = exchange(lambda j: bc_ref, bcs.at[:, me], sb, rb)
     dt_copies = exchange(lambda j: dt_ref, dts.at[:, me], sd, rd)
-    x_copies = exchange(lambda j: x_ref.at[:, :, cols(j)], xs.at[:, me], sx, rx)
-    z_copies = exchange(lambda j: z_ref.at[:, :, cols(j)], zs.at[:, me], sz, rz)
 
     w_rows = w_ref.shape[0] // n_grp
     part = me * n_rep + rep
@@ -277,6 +275,9 @@
     @pl.when(jnp.logical_not(w_self))
     def _():
         w_copy.start()
+
+    x_copies = exchange(lambda j: x_ref.at[:, :, cols(j)], xs.at[:, me], sx, rx)
+    z_copies = exchange(lambda j: z_ref.at[:, :, cols(j)], zs.at[:, me], sz, rz)
 
     begin = start_ref[0]
     live = lax.broadcasted_iota(jnp.int32, (length, LANES), 0) >= begin
@@ -318,6 +319,27 @@
         rows_t[1, c] = lax.dot_general(eye, step[r], NT, precision=highest, preferred_element_type=F32)
         raw = lax.dot_general(c_scr[r, :], b_scr[r, :], NT, preferred_element_type=F32)
         scores[c] = jnp.where(causal, raw, 0.0)
+
+    @pl.when(w_self)
+    def _():
+        pltpu.make_async_copy(w_src, w_piece(grp, head), rw).wait()
+
+    @pl.when(jnp.logical_not(w_self))
+    def _():
+        w_copy.wait()
+
+    wf_copies = []
+    for og in range(n_grp):
+        for orr in range(n_rep):
+            if og or orr:
+                slot = og * n_rep + orr
+                wf_copies.append(pltpu.make_async_remote_copy(
+                    src_ref=w_piece(grp, rep), dst_ref=w_piece(grp, rep),
+                    send_sem=swf.at[slot], recv_sem=rwf.at[slot],
+                    device_id={"grp": lax.rem(grp + og, n_grp), "rep": lax.rem(rep + orr, n_rep)},
+                    device_id_type=MESH))
+    for copy in wf_copies:
+        copy.start()
 
     for copy in x_copies:
         copy.wait()
@@ -362,7 +384,12 @@
             scaled = (jnp.exp(last - cl) * sl * xb.astype(F32)).astype(BF16)
             state = jnp.exp(last) * state + lax.dot_general(
                 b_scr[r, :], scaled, TN, preferred_element_type=F32)
-        fin[pl.ds(i * per_chunk, per_chunk)] = state.T.reshape(per_chunk, n, HEAD_DIM // n, NSTATE)
+        turned = state.T
+        piece = HEAD_DIM // n
+        for k in range(per_chunk):
+            for p in range(HEAD_DIM):
+                fin[p // piece, p % piece, pl.ds(i * per_chunk + k, 1), :] = (
+                    turned[k * HEAD_DIM + p : k * HEAD_DIM + p + 1, :])
 
     def slab_of(s):
         return jnp.minimum(sum(jnp.where(owner_ref[j] == s, j, 0) for j in range(n)), n - 1)
@@ -370,10 +397,11 @@
     f_copies = []
     for o in range(1, n):
         to = lax.rem(me + o, n)
-        fsnd[o] = fin[:, slab_of(to)]
+        fsnd[o] = fin[slab_of(to)].astype(BF16)
         f_copies.append(pltpu.make_async_remote_copy(
             src_ref=fsnd.at[o], dst_ref=frecv.at[me], send_sem=sf.at[o], recv_sem=rf.at[o],
             device_id={"seq": to}, device_id_type=MESH))
+        f_copies[-1].start()
 
     for copy in z_copies:
         copy.wait()
@@ -391,27 +419,6 @@
         r = slice(c * SPAN, (c + 1) * SPAN)
         total = jnp.broadcast_to(jnp.sum(squares[r], axis=1, keepdims=True), (SPAN, LANES))
         ssnd[c] = total.T[0:8, :]
-
-    @pl.when(w_self)
-    def _():
-        pltpu.make_async_copy(w_src, w_piece(grp, head), rw).wait()
-
-    @pl.when(jnp.logical_not(w_self))
-    def _():
-        w_copy.wait()
-
-    wf_copies = []
-    for og in range(n_grp):
-        for orr in range(n_rep):
-            if og or orr:
-                slot = og * n_rep + orr
-                wf_copies.append(pltpu.make_async_remote_copy(
-                    src_ref=w_piece(grp, rep), dst_ref=w_piece(grp, rep),
-                    send_sem=swf.at[slot], recv_sem=rwf.at[slot],
-                    device_id={"grp": lax.rem(grp + og, n_grp), "rep": lax.rem(rep + orr, n_rep)},
-                    device_id_type=MESH))
-    for copy in wf_copies:
-        copy.start()
 
     s_copies = []
     for oh in range(n_head):
@@ -423,7 +430,7 @@
                     src_ref=ssnd.at[to], dst_ref=srecv.at[slot], send_sem=ss.at[slot],
                     recv_sem=rs.at[slot],
                     device_id={"seq": to, "head": lax.rem(head + oh, n_head)}, device_id_type=MESH))
-    for copy in s_copies + f_copies:
+    for copy in s_copies:
         copy.start()
     for copy in wf_copies:
         copy.wait()
@@ -484,18 +491,24 @@
 
     slab = slab_of(me)
     tail_live = length - 16 + lax.broadcasted_iota(jnp.int32, (16, width), 0) >= begin
-    tailx_ref[...] = jnp.where(tail_live, tails[slab].astype(F32), 0.0).astype(BF16)
+    rim = KCONV - 1
+    kept = jnp.where(tail_live, tails[slab].astype(F32), 0.0)
+    tailx_ref[...] = kept[16 - rim :].astype(BF16)
     state_cols = tailbc_ref.shape[1]
     wide_bc = bcs.shape[3]
     chosen = (lax.broadcasted_iota(jnp.int32, (wide_bc, state_cols), 0)
               == slab * state_cols + lax.broadcasted_iota(jnp.int32, (wide_bc, state_cols), 1)).astype(BF16)
-    tailbc_ref[...] = jnp.dot(
-        bpad[PAD + length - 16 : PAD + length, :].astype(BF16), chosen, preferred_element_type=F32).astype(BF16)
+    kept = jnp.dot(
+        bpad[PAD + length - 16 : PAD + length, :].astype(BF16), chosen, preferred_element_type=F32)
+    tailbc_ref[...] = kept[16 - rim :].astype(BF16)
 
     for copy in f_copies:
         copy.wait()
-    frecv[me] = fin[:, slab]
-    ssm_ref[...] = frecv[...]
+    for o in range(n):
+        source = lax.rem(me + n - o, n)
+        for p in range(HEAD_DIM // n):
+            value = frecv[source, p].astype(F32) if o else fin[slab, p]
+            ssm_ref[source, :, p * NSTATE : (p + 1) * NSTATE] = value
 
     for copy in q_copies:
         copy.wait()
@@ -526,9 +539,9 @@
         functools.partial(fused_kernel, sizes),
         out_shape=(
             jax.ShapeDtypeStruct((SPAN, out_cols), BF16),
-            jax.ShapeDtypeStruct((n, own_heads, piece, NSTATE), F32),
-            jax.ShapeDtypeStruct((16, width), BF16),
-            jax.ShapeDtypeStruct((16, bc_cols // n), BF16),
+            jax.ShapeDtypeStruct((n, own_heads, piece * NSTATE), F32),
+            jax.ShapeDtypeStruct((KCONV - 1, width), BF16),
+            jax.ShapeDtypeStruct((KCONV - 1, bc_cols // n), BF16),
         ),
         in_specs=[smem, smem, hbm, hbm, hbm, hbm] + [here] * 6 + [hbm],
         out_specs=(here,) * 4,
@@ -547,9 +560,9 @@
             vmem((blocks, SPAN, SPAN), F32),
             vmem((length, width), F32),
             vmem((length, width), BF16),
-            vmem((own_heads, n, piece, NSTATE), F32),
-            vmem((n, own_heads, piece, NSTATE), F32),
-            vmem((n, own_heads, piece, NSTATE), F32),
+            vmem((n, piece, own_heads, NSTATE), F32),
+            vmem((n, piece, own_heads, NSTATE), BF16),
+            vmem((n, piece, own_heads, NSTATE), BF16),
             vmem((n, 16, width), BF16),
             vmem((width, out_cols * n_head), BF16),
             vmem((n_head - 1, blocks, SPAN, out_cols), BF16),
@@ -584,12 +597,11 @@
         norm_gain[None],
         out_weight,
     )
-    rim = KCONV - 1
     return (
         mixed[None],
         ssm.reshape(1, 1, heads, piece * NSTATE),
-        tail_x[16 - rim :][None, None],
-        tail_bc[16 - rim :][None, None],
+        tail_x[None, None],
+        tail_bc[None, None],
     )
 
 

time: 179 us -> 154 us (0.86); the launches traced: 177 us -> 154 us
  Pallas kernels: 169 us -> 147 us
    pallas_call x1, Pallas kernels: 169 us -> 147 us  [fused(): pl.pallas_call(functools.partial(fused_kernel, sizes), out_shape=(jax.Sha...]
    unnamed x1 -> x4, local copies, waits for them, and re-layouts: 1.67 us -> 6.06 us
    broadcast_in_dim x2 -> x0, local copies, waits for them, and re-layouts: 2.56 us -> none  [the longest x1 1.32 us: fused(): tail_x[16 - rim:][None, None]]
    reshape x1 -> x0, local copies, waits for them, and re-layouts: 1.92 us -> none  [fused(): ssm.reshape(1, 1, heads, piece * NSTATE)]
where the time goes in v2:
time: 154 us
  Pallas kernels  147 us (95%)
  local copies, waits for them, and re-layouts  6.06 us (4%)
    pallas_call x1, Pallas kernels, fused(): pl.pallas_call(functools.partial(fused_kernel, sizes), out_shape=(jax.Sha...  147 us
    unnamed x4, local copies, waits for them, and re-layouts  6.06 us

profile of v2, /device:TPU:0, one launch (start us, length us, event | category | flops | bytes accessed | tf_op | source)
XLA Modules:
  0.0 154.0 jit_solution(2863434420796996284)
XLA Ops:
  1.3 146.7 %shard_map.156 = (bf16[128,1024]{1,0:T(8,128)(2,1)}, f32[4,16,2048]{2,1,0:T(8,128)}, bf16[3,1024]{1,0:T(4,128)(2,1)}, bf16[3,64]{1,0:T(4,128)(2,1)}) custom-call(s32[1]{0:T(128)S(6)} %copy.21.start_ref, s32[4]{0:T(128)} %bitcast.22, bf16[4,32,4096]{2,1,0:T(8,128)(2,1)} %bitcast.13, bf16[4,32,4096]{2,1,0:T(8,128)(2,1)} %bitcast.14, ...), custom_call_target="tpu_custom_call" | custom-call | tf_op jit(solution)/shard_map/pallas_call | solution.py:538
  148.0 1.7 %copy.22 = bf16[1,128,1024]{2,1,0:T(8,128)(2,1)} copy(bf16[1,128,1024]{2,1,0:T(8,128)(2,1)} %bitcast.16) | data formatting | bytes 524288
  149.6 1.9 %copy.23 = f32[1,1,64,2048]{3,2,1,0:T(8,128)} copy(f32[1,1,64,2048]{3,2,1,0:T(8,128)} %bitcast.15) | data formatting | bytes 1048576
  151.5 1.3 copy.24
  152.8 1.2 copy.25

commit v3 on v2

--- a/solution.py
+++ b/solution.py
@@ -254,6 +254,8 @@
     bc_copies = exchange(lambda j: bc_ref, bcs.at[:, me], sb, rb)
     dt_copies = exchange(lambda j: dt_ref, dts.at[:, me], sd, rd)
 
+    x_copies = exchange(lambda j: x_ref.at[:, :, cols(j)], xs.at[:, me], sx, rx)
+
     w_rows = w_ref.shape[0] // n_grp
     part = me * n_rep + rep
     to_seq, to_head, to_rep = lax.rem(part, n), part // n, head
@@ -276,7 +278,6 @@
     def _():
         w_copy.start()
 
-    x_copies = exchange(lambda j: x_ref.at[:, :, cols(j)], xs.at[:, me], sx, rx)
     z_copies = exchange(lambda j: z_ref.at[:, :, cols(j)], zs.at[:, me], sz, rz)
 
     begin = start_ref[0]
@@ -320,27 +321,6 @@
         raw = lax.dot_general(c_scr[r, :], b_scr[r, :], NT, preferred_element_type=F32)
         scores[c] = jnp.where(causal, raw, 0.0)
 
-    @pl.when(w_self)
-    def _():
-        pltpu.make_async_copy(w_src, w_piece(grp, head), rw).wait()
-
-    @pl.when(jnp.logical_not(w_self))
-    def _():
-        w_copy.wait()
-
-    wf_copies = []
-    for og in range(n_grp):
-        for orr in range(n_rep):
-            if og or orr:
-                slot = og * n_rep + orr
-                wf_copies.append(pltpu.make_async_remote_copy(
-                    src_ref=w_piece(grp, rep), dst_ref=w_piece(grp, rep),
-                    send_sem=swf.at[slot], recv_sem=rwf.at[slot],
-                    device_id={"grp": lax.rem(grp + og, n_grp), "rep": lax.rem(rep + orr, n_rep)},
-                    device_id_type=MESH))
-    for copy in wf_copies:
-        copy.start()
-
     for copy in x_copies:
         copy.wait()
     tail_src = xs.at[nb - 1, n - 1, sub - 16 : sub, :]
@@ -348,8 +328,7 @@
 
     left = lax.broadcasted_iota(jnp.int32, (SPAN, LANES), 1) < HEAD_DIM
 
-    @pl.loop(0, width // LANES)
-    def _(i):
+    def chunk(i):
         lanes = pl.ds(pl.multiple_of(i * LANES, LANES), LANES)
         wide = pl.ds(pl.multiple_of(me * width + i * LANES, LANES), LANES)
         xv = xs[:, :, :, lanes].reshape(length, LANES).astype(F32)
@@ -391,6 +370,41 @@
                 fin[p // piece, p % piece, pl.ds(i * per_chunk + k, 1), :] = (
                     turned[k * HEAD_DIM + p : k * HEAD_DIM + p + 1, :])
 
+    half = width // LANES // 2
+    pl.loop(0, half)(chunk)
+
+    @pl.when(w_self)
+    def _():
+        pltpu.make_async_copy(w_src, w_piece(grp, head), rw).wait()
+
+    @pl.when(jnp.logical_not(w_self))
+    def _():
+        w_copy.wait()
+
+    def forward(piece_grp, og, orr, to):
+        slot = og * n_rep + orr
+        piece = w_piece(piece_grp, rep)
+        return pltpu.make_async_remote_copy(
+            src_ref=piece, dst_ref=piece, send_sem=swf.at[slot], recv_sem=rwf.at[slot],
+            device_id=to, device_id_type=MESH)
+
+    over_grp = [forward(grp, og, 0, {"grp": lax.rem(grp + og, n_grp)}) for og in range(1, n_grp)]
+    over_rep = [forward(grp, 0, o, {"rep": lax.rem(rep + o, n_rep)}) for o in range(1, n_rep)]
+    for copy in over_grp + over_rep:
+        copy.start()
+
+    pl.loop(half, width // LANES)(chunk)
+
+    for copy in over_grp:
+        copy.wait()
+    again = [
+        forward(lax.rem(grp + n_grp - og, n_grp), og, o, {"rep": lax.rem(rep + o, n_rep)})
+        for og in range(1, n_grp)
+        for o in range(1, n_rep)
+    ]
+    for copy in again:
+        copy.start()
+
     def slab_of(s):
         return jnp.minimum(sum(jnp.where(owner_ref[j] == s, j, 0) for j in range(n)), n - 1)
 
@@ -432,7 +446,7 @@
                     device_id={"seq": to, "head": lax.rem(head + oh, n_head)}, device_id_type=MESH))
     for copy in s_copies:
         copy.start()
-    for copy in wf_copies:
+    for copy in over_rep + again:
         copy.wait()
 
     tile = 256 if out_cols % 256 == 0 else LANES

time: 154 us -> 147 us (0.955)
  Pallas kernels: 147 us -> 140 us
    pallas_call x1, Pallas kernels: 147 us -> 140 us  [fused(): pl.pallas_call(functools.partial(fused_kernel, sizes), out_shape=(jax.Sha...]
where the time goes in v3:
time: 147 us
  Pallas kernels  140 us (95%)
  local copies, waits for them, and re-layouts  6.06 us (4%)
    pallas_call x1, Pallas kernels, fused(): pl.pallas_call(functools.partial(fused_kernel, sizes), out_shape=(jax.Sha...  140 us
    unnamed x4, local copies, waits for them, and re-layouts  6.06 us

profile of v3, /device:TPU:0, one launch (start us, length us, event | category | flops | bytes accessed | tf_op | source)
XLA Modules:
  0.0 147.1 jit_solution(3273424919353966778)
XLA Ops:
  1.3 139.7 %shard_map.156 = (bf16[128,1024]{1,0:T(8,128)(2,1)}, f32[4,16,2048]{2,1,0:T(8,128)}, bf16[3,1024]{1,0:T(4,128)(2,1)}, bf16[3,64]{1,0:T(4,128)(2,1)}) custom-call(s32[1]{0:T(128)S(6)} %copy.21.start_ref, s32[4]{0:T(128)} %bitcast.22, bf16[4,32,4096]{2,1,0:T(8,128)(2,1)} %bitcast.13, bf16[4,32,4096]{2,1,0:T(8,128)(2,1)} %bitcast.14, ...), custom_call_target="tpu_custom_call" | custom-call | tf_op jit(solution)/shard_map/pallas_call | solution.py:552
  141.0 1.7 %copy.22 = bf16[1,128,1024]{2,1,0:T(8,128)(2,1)} copy(bf16[1,128,1024]{2,1,0:T(8,128)(2,1)} %bitcast.16) | data formatting | bytes 524288
  142.7 1.9 %copy.23 = f32[1,1,64,2048]{3,2,1,0:T(8,128)} copy(f32[1,1,64,2048]{3,2,1,0:T(8,128)} %bitcast.15) | data formatting | bytes 1048576
  144.6 1.3 copy.24
  145.9 1.2 copy.25
